TPU v7x, 32 devices: a whole 2x2x4 slice. The times are simulated.
32 devices in a mesh: row: 4 (over z), col: 4 (over y, x), layer: 2 (over core).
Axes of the slice: x: 2, y: 2, z: 4, core: 2. Of those that a mesh axis runs over, the one named last changes fastest.
Arguments:
- expression: bfloat16 [6144, 1024], P(('row', 'col'), 'layer'), may hold values from -240 to 240
Outputs:
- connectivity: float32 [6144], P(('row', 'col', 'layer'))
All inputs are finite; a program needn't handle non-finite values.
Results may differ from a plain program's by a relative error of at most 0.00048.
Values may be sent and summed in bfloat16 or wider, within the bound.
A program may use at most 64 MiB of HBM per device.

v0:
```python
import jax
import jax.numpy as jnp
from jax import lax
from jax.sharding import PartitionSpec as P

S = 1024
epsilon = 1e-05


def adjacency(correlation):
    shifted = (1.0 + correlation) * 0.5
    square = shifted * shifted
    fourth = square * square
    eighth = fourth * fourth
    return eighth * fourth


def standardize(values, total, squares):
    average = total / S
    variance = squares / S - average * average
    return ((values - average[:, None]) * lax.rsqrt(variance + epsilon)[:, None]).astype(
        jnp.bfloat16
    )


def pair_products(left, right):
    return lax.dot_general(
        left, right, (((1,), (1,)), ((), ())), preferred_element_type=jnp.float32
    )


def on_device(expression):
    whole = lax.all_gather(expression, "layer", axis=1, tiled=True)
    values = whole.astype(jnp.float32)
    scaled = standardize(values, jnp.sum(values, axis=1), jnp.sum(values * values, axis=1))
    row_genes = lax.all_gather(scaled, "col", axis=0, tiled=True)
    share = scaled.shape[0] // lax.axis_size("layer")
    own_half = lax.dynamic_slice_in_dim(scaled, lax.axis_index("layer") * share, share, 0)
    partial_value = jnp.sum(
        adjacency(
            pair_products(lax.all_gather(own_half, "row", axis=0, tiled=True), row_genes) / S
        ),
        axis=0,
    )
    summed = lax.psum_scatter(partial_value, ("col", "layer"), scatter_dimension=0, tiled=True)
    return summed - 1.0


def solution(mesh):
    placed = (P(("row", "col"), "layer"),)
    return jax.shard_map(
        on_device, mesh=mesh, in_specs=placed, out_specs=P(("row", "col", "layer")), check_vma=False
    )
```

profile of v0, /device:TPU:0, one launch (start us, length us, event | category | flops | bytes accessed | tf_op | source)
XLA Modules:
  0.0 121.1 jit_solution(8612865280336026909)
XLA Ops:
  6.5 0.0 copy-start.1
  6.5 0.0 all-gather.3.cloned.1.call-start
  6.5 2.8 %all_gather.9 = bf16[384,1024]{1,0:T(8,128)(2,1)S(1)} all-gather(bf16[384,512]{1,0:T(8,128)(2,1)} %param.1), channel_id=1, replica_groups=mesh['row'=4,'col'=4,'layer'=2] {'layer'}, dimensions={1}, use_global_device_ids=true | all-gather | bytes 1179648 | tf_op jit(solution)/shard_map/all_gather | solution.py:33
  9.4 0.3 convert_reduce_fusion
  9.7 0.3 fusion.2
  9.9 0.0 copy-start
  10.0 0.9 constant_dynamic-slice_fusion
  10.8 0.0 all-gather.3.cloned.1.call-update
  10.8 0.0 all-gather.5.cloned.1.call-start
  10.9 0.1 copy-done
  11.0 0.6 all-gather.5.cloned.1.call-update
  11.6 0.0 copy-done.1
  11.6 0.6 dynamic-slice
  12.8 37.8 %all-gather.3.cloned.1.call-done = bf16[768,1024]{1,0:T(8,128)(2,1)} async-done(((bf16[192,1024]{1,0:T(8,128)(2,1)}), bf16[768,1024]{1,0:T(8,128)(2,1)}) %all-gather.3.cloned.1.call-update) | async-done | bytes 1572880 | tf_op jit(solution)/shard_map/all_gather | solution.py:41
  50.6 44.6 %all-gather.5.cloned.1.call-done = bf16[1536,1024]{1,0:T(8,128)(2,1)} async-done(((bf16[384,1024]{1,0:T(8,128)(2,1)}), bf16[1536,1024]{1,0:T(8,128)(2,1)}) %all-gather.5.cloned.1.call-update) | async-done | bytes 3145744 | tf_op jit(solution)/shard_map/all_gather | solution.py:36
  95.2 5.6 %fusion = f32[1536]{0:T(1024)S(1)} fusion(bf16[768,1024]{1,0:T(8,128)(2,1)} %all-gather.3.cloned.1.call-done, bf16[1536,1024]{1,0:T(8,128)(2,1)} %all-gather.5.cloned.1.call-done), kind=kOutput, calls=%fused_computation.1 | convolution fusion | flops 2425354752 | bytes 4724736 | tf_op jit(solution)/shard_map/dot_general | solution.py:27
  100.8 12.8 %all-reduce = f32[1536]{0:T(1024)S(1)} all-reduce(f32[1536]{0:T(1024)S(1)} %fusion), channel_id=2, replica_groups=mesh['row'=4,'col'=4,'layer'=2] {'col','layer'}, use_global_device_ids=true, to_apply=%region_3.0.clone | all-reduce | flops 1536 | bytes 12288
  113.6 0.6 dynamic-slice_add_fusion
  (1 shorter events, 0.0 us)
Async XLA Ops:
  6.5 5.1 %copy-start.1 = (u32[32]{0:T(128)S(1)}, u32[32]{0:T(128)}, u32[]{:S(2)}) copy-start(u32[32]{0:T(128)} %constant.29) | copy-start | bytes 388
  6.5 44.1 %all-gather.3.cloned.1.call-start = ((), (), s32[]{:S(2)}) async-start(), calls=%async_computation | async-start | bytes 1966080 | tf_op jit(solution)/shard_map/all_gather | solution.py:41
  9.9 1.1 copy-start
  10.8 84.4 %all-gather.5.cloned.1.call-start = ((), (), s32[]{:S(2)}) async-start(), calls=%async_computation.1 | async-start | bytes 3932160 | tf_op jit(solution)/shard_map/all_gather | solution.py:36
Sparse Core Ops, SparseCore 0:
  11.0 39.6 all-gather.2
  52.5 42.6 all-gather.4
where the time goes:
time: 121 us
  waiting for transfers between devices  83 us (69%)
  blocking collectives  15.6 us (13%)
  between operations  14.1 us (12%)
  matrix products  5.59 us (5%)
  local copies, waits for them, and re-layouts  1.56 us (1%)
  other arithmetic  1.22 us (1%)
    all_gather x1, waiting for transfers between devices, on_device(): row_genes = lax.all_gather(scaled, 'col', axis=0, tiled=True)  44.6 us
    all_gather x1, waiting for transfers between devices, on_device(): lax.all_gather(own_half, 'row', axis=0, tiled=True)  37.8 us
    unnamed x1, blocking collectives  12.8 us
    dot_general x1, matrix products, pair_products(): lax.dot_general(left, right, (((1,), (1,)), ((), ())), preferred_element_...  5.59 us
    all_gather x1, blocking collectives, on_device(): whole = lax.all_gather(expression, 'layer', axis=1, tiled=True)  2.82 us
  transfers between devices with their start and end apart: 2, of which 2 were waited for; matrix products, arithmetic and copies ran while one was open for 0% of the time, Pallas kernels for 0%

commit v1 on v0

--- a/solution.py
+++ b/solution.py
@@ -5,6 +5,16 @@
 
 S = 1024
 epsilon = 1e-05
+
+
+def around_the_ring(x, axis, along):
+    size = lax.axis_size(axis)
+    held, blocks = (x, [x])
+    for _ in range(size - 1):
+        held = lax.ppermute(held, axis, [(i, (i + 1) % size) for i in range(size)])
+        blocks.insert(0, held)
+    flat = jnp.concatenate(blocks, axis=along)
+    return jnp.roll(flat, (lax.axis_index(axis) + 1) * x.shape[along], axis=along)
 
 
 def adjacency(correlation):
@@ -33,7 +43,7 @@
     whole = lax.all_gather(expression, "layer", axis=1, tiled=True)
     values = whole.astype(jnp.float32)
     scaled = standardize(values, jnp.sum(values, axis=1), jnp.sum(values * values, axis=1))
-    row_genes = lax.all_gather(scaled, "col", axis=0, tiled=True)
+    row_genes = around_the_ring(scaled, "col", 0)
     share = scaled.shape[0] // lax.axis_size("layer")
     own_half = lax.dynamic_slice_in_dim(scaled, lax.axis_index("layer") * share, share, 0)
     partial_value = jnp.sum(

time: 121 us -> 104 us (0.86)
  waiting for transfers between devices: 83 us -> 55.1 us
  local copies, waits for them, and re-layouts: 1.56 us -> 6.99 us
  starting transfers between devices: 0.04 us -> 3.69 us
  other arithmetic: 1.22 us -> 3.55 us
    ppermute x0 -> x3, waiting for transfers between devices: none -> 55 us  [around_the_ring(): held = lax.ppermute(held, axis, [(i, (i + 1) % size) for i in range(size)])]
    all_gather x1 -> x0, waiting for transfers between devices: 44.6 us -> none  [on_device(): row_genes = lax.all_gather(scaled, 'col', axis=0, tiled=True)]
    all_gather x1, waiting for transfers between devices: 37.8 us -> 0.01 us  [on_device(): lax.all_gather(own_half, 'row', axis=0, tiled=True)]
    unnamed x5 -> x9, local copies, waits for them, and re-layouts: 0.7 us -> 6.22 us
    ppermute x0 -> x3, starting transfers between devices: none -> 3.69 us  [around_the_ring(): held = lax.ppermute(held, axis, [(i, (i + 1) % size) for i in range(size)])]
  transfers between devices with their start and end apart: 2 -> 4, of which waited for: 2 -> 3; matrix products, arithmetic and copies ran while one was open for 0% -> 9% of each run, Pallas kernels for 0% -> 0%
where the time goes in v1:
time: 104 us
  waiting for transfers between devices  55.1 us (53%)
  blocking collectives  14.9 us (14%)
  between operations  14.1 us (14%)
  local copies, waits for them, and re-layouts  6.99 us (7%)
  matrix products  5.74 us (6%)
  starting transfers between devices  3.69 us (4%)
  other arithmetic  3.55 us (3%)
    ppermute x3, waiting for transfers between devices, around_the_ring(): held = lax.ppermute(held, axis, [(i, (i + 1) % size) for i in range(size)])  55 us
    unnamed x1, blocking collectives  12 us
    unnamed x9, local copies, waits for them, and re-layouts  6.22 us
    dot_general x1, matrix products, pair_products(): lax.dot_general(left, right, (((1,), (1,)), ((), ())), preferred_element_...  5.74 us
    ppermute x3, starting transfers between devices, around_the_ring(): held = lax.ppermute(held, axis, [(i, (i + 1) % size) for i in range(size)])  3.69 us
    all_gather x1, blocking collectives, on_device(): whole = lax.all_gather(expression, 'layer', axis=1, tiled=True)  2.82 us
  transfers between devices with their start and end apart: 4, of which 3 were waited for; matrix products, arithmetic and copies ran while one was open for 9% of the time, Pallas kernels for 0%

profile of v1, /device:TPU:0, one launch (start us, length us, event | category | flops | bytes accessed | tf_op | source)
XLA Modules:
  0.0 104.0 jit_solution(6751957552784910214)
XLA Ops:
  6.5 0.0 copy-start
  6.5 0.0 all-gather.2.cloned.1.call-start
  6.5 2.8 %all_gather.6 = bf16[384,1024]{1,0:T(8,128)(2,1)S(1)} all-gather(bf16[384,512]{1,0:T(8,128)(2,1)} %param.1), channel_id=1, replica_groups=mesh['row'=4,'col'=4,'layer'=2] {'layer'}, dimensions={1}, use_global_device_ids=true | all-gather | bytes 1179648 | tf_op jit(solution)/shard_map/all_gather | solution.py:43
  9.4 0.3 convert_reduce_fusion
  9.7 0.3 fusion.3
  9.9 2.9 %collective-permute-start = (bf16[384,1024]{1,0:T(8,128)(2,1)S(1)}, bf16[384,1024]{1,0:T(8,128)(2,1)S(1)}, u32[]{:S(2)}, u32[]{:S(2)}) collective-permute-start(bf16[384,1024]{1,0:T(8,128)(2,1)S(1)} %fusion.3), channel_id=1, source_target_pairs={{0,2},{2,4},{4,6},{6,0},{1,3},{3,5},{5,7},{7,1},{8,10},{10,12},{12... | collective-permute-start | bytes 2359304 | tf_op jit(solution)/shard_map/ppermute | solution.py:14
  12.8 18.8 %collective-permute-done = bf16[384,1024]{1,0:T(8,128)(2,1)S(1)} collective-permute-done((bf16[384,1024]{1,0:T(8,128)(2,1)S(1)}, bf16[384,1024]{1,0:T(8,128)(2,1)S(1)}, u32[]{:S(2)}, u32[]{:S(2)}) %collective-permute-start) | collective-permute-done | bytes 786464 | tf_op jit(solution)/shard_map/ppermute | solution.py:14
  31.6 0.8 collective-permute-start.1
  32.4 0.8 constant_dynamic-slice_fusion
  33.2 0.0 all-gather.2.cloned.1.call-update
  33.2 18.3 %collective-permute-done.1 = bf16[384,1024]{1,0:T(8,128)(2,1)S(1)} collective-permute-done((bf16[384,1024]{1,0:T(8,128)(2,1)S(1)}, bf16[384,1024]{1,0:T(8,128)(2,1)S(1)}, u32[]{:S(2)}, u32[]{:S(2)}) %collective-permute-start.1) | collective-permute-done | bytes 786464 | tf_op jit(solution)/shard_map/ppermute | solution.py:14
  51.6 0.0 collective-permute-start.2
  51.6 0.0 copy-done
  51.6 0.6 dynamic-slice
  52.8 17.9 %collective-permute-done.2 = bf16[384,1024]{1,0:T(8,128)(2,1)S(1)} collective-permute-done((bf16[384,1024]{1,0:T(8,128)(2,1)S(1)}, bf16[384,1024]{1,0:T(8,128)(2,1)S(1)}, u32[]{:S(2)}, u32[]{:S(2)}) %collective-permute-start.2) | collective-permute-done | bytes 786464 | tf_op jit(solution)/shard_map/ppermute | solution.py:14
  70.7 0.9 constant_dynamic-update-slice_fusion.7
  71.6 1.0 constant_dynamic-update-slice_fusion.6
  72.6 0.9 constant_dynamic-update-slice_fusion.5
  73.5 1.1 %constant_dynamic-update-slice_fusion.4 = bf16[3072,1024]{1,0:T(8,128)(2,1)} fusion(bf16[3072,1024]{1,0:T(8,128)(2,1)} %constant_dynamic-update-slice_fusion.5, f32[384]{0:T(512)S(1)} %get-tuple-element.8, f32[384]{0:T(512)S(1)} %get-tuple-element.7, bf16[384,1024]{1,0:T(8,128)(2,1)S(1)} %all_gather.6), kind=kLoop, calls=%fused_computation.13 | loop fusion | flops 1572864 | bytes 1575936
  74.7 0.9 constant_dynamic-update-slice_fusion.3
  75.6 0.9 constant_dynamic-update-slice_fusion.2
  76.5 0.9 constant_dynamic-update-slice_fusion.1
  77.5 1.2 %constant_dynamic-update-slice_fusion = bf16[3072,1024]{1,0:T(8,128)(2,1)} fusion(bf16[3072,1024]{1,0:T(8,128)(2,1)} %constant_dynamic-update-slice_fusion.1, f32[384]{0:T(512)S(1)} %get-tuple-element.8, f32[384]{0:T(512)S(1)} %get-tuple-element.7, bf16[384,1024]{1,0:T(8,128)(2,1)S(1)} %all_gather.6), kind=kLoop, calls=%fused_computation.9 | loop fusion | flops 1572864 | bytes 1575936 | tf_op jit(solution)/shard_map/jit(_roll_dynamic)/concatenate | solution.py:17
  78.7 0.0 all-gather.2.cloned.1.call-done
  78.7 5.7 %fusion = f32[1536]{0:T(1024)S(1)} fusion(bf16[768,1024]{1,0:T(8,128)(2,1)} %all-gather.2.cloned.1.call-done, bf16[3072,1024]{1,0:T(8,128)(2,1)} %constant_dynamic-update-slice_fusion, s32[]{:T(128)S(6)} %select_n.18), kind=kOutput, calls=%fused_computation.1 | convolution fusion | flops 2425354752 | bytes 4724740 | tf_op jit(solution)/shard_map/dot_general | solution.py:37
  84.4 12.0 %all-reduce = f32[1536]{0:T(1024)S(1)} all-reduce(f32[1536]{0:T(1024)S(1)} %fusion), channel_id=2, replica_groups=mesh['row'=4,'col'=4,'layer'=2] {'col','layer'}, use_global_device_ids=true, to_apply=%region_3.4.clone | all-reduce | flops 1536 | bytes 12288
  96.5 0.6 dynamic-slice_add_fusion
  (1 shorter events, 0.0 us)
Async XLA Ops:
  6.5 45.0 %copy-start = (u32[32]{0:T(128)S(1)}, u32[32]{0:T(128)}, u32[]{:S(2)}) copy-start(u32[32]{0:T(128)} %constant.53) | copy-start | bytes 388
  6.5 72.1 %all-gather.2.cloned.1.call-start = ((), (), s32[]{:S(2)}) async-start(), calls=%async_computation | async-start | bytes 1966080 | tf_op jit(solution)/shard_map/all_gather | solution.py:51
  9.9 21.7 %collective-permute-start = (bf16[384,1024]{1,0:T(8,128)(2,1)S(1)}, bf16[384,1024]{1,0:T(8,128)(2,1)S(1)}, u32[]{:S(2)}, u32[]{:S(2)}) collective-permute-start(bf16[384,1024]{1,0:T(8,128)(2,1)S(1)} %fusion.3), channel_id=1, source_target_pairs={{0,2},{2,4},{4,6},{6,0},{1,3},{3,5},{5,7},{7,1},{8,10},{10,12},{12... | collective-permute-start | bytes 2359304 | tf_op jit(solution)/shard_map/ppermute | solution.py:14
  31.6 19.9 %collective-permute-start.1 = (bf16[384,1024]{1,0:T(8,128)(2,1)S(1)}, bf16[384,1024]{1,0:T(8,128)(2,1)S(1)}, u32[]{:S(2)}, u32[]{:S(2)}) collective-permute-start(bf16[384,1024]{1,0:T(8,128)(2,1)S(1)} %collective-permute-done), channel_id=1, source_target_pairs={{0,2},{2,4},{4,6},{6,0},{1,3},{3,5},{5,7},{7,1},{8,10},{10,12},{12... | collective-permute-start | bytes 2359304 | tf_op jit(solution)/shard_map/ppermute | solution.py:14
  51.6 19.2 %collective-permute-start.2 = (bf16[384,1024]{1,0:T(8,128)(2,1)S(1)}, bf16[384,1024]{1,0:T(8,128)(2,1)S(1)}, u32[]{:S(2)}, u32[]{:S(2)}) collective-permute-start(bf16[384,1024]{1,0:T(8,128)(2,1)S(1)} %collective-permute-done.1), channel_id=1, source_target_pairs={{0,2},{2,4},{4,6},{6,0},{1,3},{3,5},{5,7},{7,1},{8,10},{10,12},{12... | collective-permute-start | bytes 2359304 | tf_op jit(solution)/shard_map/ppermute | solution.py:14
Sparse Core Ops, SparseCore 0:
  33.3 38.2 all-gather.1
